TPU v7x, 32 devices: a whole 2x2x4 slice. The times are simulated.
32 devices in a mesh: grp: 4 (over y, x), dev: 8 (over z, core).
Axes of the slice: x: 2, y: 2, z: 4, core: 2. Of those that a mesh axis runs over, the one named last changes fastest.
Arguments:
- points: bfloat16 [65536, 256], P(('grp', 'dev')), may hold values from -6 to 6
- ridge: float32 [1024], replicated, may hold values from 0.25 to 2
- landmark_ids: int32 [1024], replicated, may hold values from 0 to 65535, as said below
Outputs:
- features: bfloat16 [65536, 1024], P(('grp', 'dev'))
Inputs may be any that keep to these rules, and one draw needn't show every extreme that they name: `landmark_ids`: sorted ascending, all distinct.
All inputs are finite; a program needn't handle non-finite values.
Results may differ from a plain program's by a relative error of at most 0.0015.
Values may be sent and summed in bfloat16 or wider, within the bound.
No kernel may reach another device: no remote copies, remote signals or barrier semaphores. Data moves between devices by JAX's collectives and lax.ppermute only.
A program may use at most 128 MiB of HBM per device.

v0:
```python
import jax
import jax.numpy as jnp
from jax import lax
from jax.sharding import PartitionSpec as P


def kernel_block(left, right):
    left_sq = jnp.sum(jnp.square(left.astype(jnp.float32)), axis=1)
    right_sq = jnp.sum(jnp.square(right.astype(jnp.float32)), axis=1)
    inner = jnp.dot(left, right.T, preferred_element_type=jnp.float32)
    width = left.shape[1]
    return jnp.exp(-(left_sq[:, None] + right_sq[None, :] - 2.0 * inner) / (2.0 * width))


def shards(points, ridge, landmark_ids):
    count = points.shape[0]
    start = lax.axis_index(("grp", "dev")) * count
    offset = landmark_ids - start
    inside = (offset >= 0) & (offset < count)
    picked = points[jnp.clip(offset, 0, count - 1)]
    filled = jnp.where(inside[:, None], picked.astype(jnp.float32), 0.0)
    marks = lax.psum(filled, ("grp", "dev")).astype(jnp.bfloat16)
    core = kernel_block(marks, marks) + jnp.diag(ridge)
    lower = jnp.linalg.cholesky(core)
    cross = kernel_block(points, marks)
    raw = lax.linalg.triangular_solve(lower, cross, left_side=False, lower=True, transpose_a=True)
    total_rows = count * lax.axis_size(("grp", "dev"))
    totals, squares = lax.psum(
        (jnp.sum(raw, axis=0), jnp.sum(jnp.square(raw), axis=0)), ("grp", "dev")
    )
    mean = totals / total_rows
    var = jnp.maximum(squares / total_rows - jnp.square(mean), 0.0)
    centered = raw - mean[None, :]
    return (centered / jnp.sqrt(var + 1e-05)[None, :]).astype(jnp.bfloat16)


def solution(mesh):
    placed = (P(("grp", "dev"), None), P(), P())
    return jax.shard_map(
        shards, mesh=mesh, in_specs=placed, out_specs=P(("grp", "dev"), None), check_vma=False
    )
```

profile of v0, /device:TPU:0, one launch (start us, length us, event | category | flops | bytes accessed | tf_op | source)
XLA Modules:
  0.0 495.3 jit_solution(2860757767389505931)
XLA Ops:
  8.1 53.3 %all-reduce.3 = bf16[1024,256]{1,0:T(8,128)(2,1)S(1)} all-reduce(f32[1024,256]{1,0:T(8,128)S(1)} %convert_select_fusion), channel_id=1, replica_groups=mesh['grp'=4,'dev'=8] {'grp','dev'}, use_global_device_ids=true, to_apply=%region_1.2 | all-reduce | flops 262144 | bytes 1572864 | tf_op jit(solution)/shard_map/psum | solution.py:22
  66.0 5.6 %subtract_negate_fusion = (f32[1024,1024]{0,1:T(8,128)}, f32[1024,1024]{0,1:T(8,128)}, f32[1024,1024]{0,1:T(8,128)}) fusion(f32[1024]{0:T(1024)S(1)} %multiply_reduce_fusion.2, bf16[1024,256]{1,0:T(8,128)(2,1)S(1)} %all-reduce.3), kind=kOutput, calls=%fused_computation.27 | convolution fusion | flops 541065216 | bytes 13111296 | tf_op jit(solution)/shard_map/dot_general | solution.py:10
  71.6 5.4 %copy.5 = f32[1024,1024]{1,0:T(8,128)} copy(f32[1024,1024]{0,1:T(8,128)} %get-tuple-element.76) | data formatting | bytes 8388608 | tf_op jit(solution)/shard_map/neg | solution.py:12
  82.3 6.3 %fusion.16 = f32[1024,1024]{1,0:T(8,128)S(1)} fusion(f32[1024,1024]{1,0:T(8,128)} %copy.6, f32[1024,1024]{1,0:T(8,128)} %copy.5, f32[1024,1024]{0,1:T(8,128)} %get-tuple-element.78, f32[1024]{0:T(1024)S(1)} %copy-done.5), kind=kLoop, calls=%fused_computation.24 | loop fusion | flops 13631488 | bytes 16781312 | tf_op jit(solution)/shard_map/jit(cholesky)/div | solution.py:24
  90.6 11.7 %cholesky.222 = f32[128,128]{1,0:T(8,128)S(1)} custom-call(f32[128,128]{1,0:T(8,128)S(1)} %cholesky.577), custom_call_target="Cholesky" | custom-call | tf_op jit(solution)/shard_map/jit(cholesky)/cholesky | solution.py:24
  102.4 9.8 %custom-call.62 = f32[1,128,128]{1,2,0:T(8,128)S(1)} custom-call(f32[1,128,128]{2,1,0:T(8,128)S(1)} %get-tuple-element.73), custom_call_target="InvertDiagBlocksLowerTriangular" | custom-call | tf_op jit(solution)/shard_map/jit(cholesky)/cholesky | solution.py:24
  118.6 11.7 %cholesky.243 = f32[128,128]{1,0:T(8,128)S(1)} custom-call(f32[128,128]{1,0:T(8,128)S(1)} %cholesky.581), custom_call_target="Cholesky" | custom-call | tf_op jit(solution)/shard_map/jit(cholesky)/cholesky | solution.py:24
  132.9 10.2 %custom-call.63 = f32[1,128,128]{1,2,0:T(8,128)S(1)} custom-call(f32[1,128,128]{2,1,0:T(8,128)S(1)} %get-tuple-element.70), custom_call_target="InvertDiagBlocksLowerTriangular" | custom-call | tf_op jit(solution)/shard_map/jit(cholesky)/cholesky | solution.py:24
  146.4 11.7 %cholesky.466 = f32[128,128]{1,0:T(8,128)S(1)} custom-call(f32[128,128]{1,0:T(8,128)S(1)} %cholesky.586), custom_call_target="Cholesky" | custom-call | tf_op jit(solution)/shard_map/jit(cholesky)/cholesky | solution.py:24
  160.1 9.8 %custom-call.64 = f32[1,128,128]{1,2,0:T(8,128)S(1)} custom-call(f32[1,128,128]{2,1,0:T(8,128)S(1)} %get-tuple-element.67), custom_call_target="InvertDiagBlocksLowerTriangular" | custom-call | tf_op jit(solution)/shard_map/jit(cholesky)/cholesky | solution.py:24
  173.4 11.9 %cholesky.485 = f32[128,128]{1,0:T(8,128)S(1)} custom-call(f32[128,128]{1,0:T(8,128)S(1)} %cholesky.591), custom_call_target="Cholesky" | custom-call | tf_op jit(solution)/shard_map/jit(cholesky)/cholesky | solution.py:24
  187.2 9.8 %custom-call.65 = f32[1,128,128]{1,2,0:T(8,128)S(1)} custom-call(f32[1,128,128]{2,1,0:T(8,128)S(1)} %get-tuple-element.64), custom_call_target="InvertDiagBlocksLowerTriangular" | custom-call | tf_op jit(solution)/shard_map/jit(cholesky)/cholesky | solution.py:24
  200.4 11.7 %cholesky.504 = f32[128,128]{1,0:T(8,128)S(1)} custom-call(f32[128,128]{1,0:T(8,128)S(1)} %cholesky.596), custom_call_target="Cholesky" | custom-call | tf_op jit(solution)/shard_map/jit(cholesky)/cholesky | solution.py:24
  214.0 9.8 %custom-call.66 = f32[1,128,128]{1,2,0:T(8,128)S(1)} custom-call(f32[1,128,128]{2,1,0:T(8,128)S(1)} %get-tuple-element.61), custom_call_target="InvertDiagBlocksLowerTriangular" | custom-call | tf_op jit(solution)/shard_map/jit(cholesky)/cholesky | solution.py:24
  227.4 11.7 %cholesky.524 = f32[128,128]{1,0:T(8,128)S(1)} custom-call(f32[128,128]{1,0:T(8,128)S(1)} %cholesky.601), custom_call_target="Cholesky" | custom-call | tf_op jit(solution)/shard_map/jit(cholesky)/cholesky | solution.py:24
  241.0 9.8 %custom-call.67 = f32[1,128,128]{1,2,0:T(8,128)S(1)} custom-call(f32[1,128,128]{2,1,0:T(8,128)S(1)} %get-tuple-element.58), custom_call_target="InvertDiagBlocksLowerTriangular" | custom-call | tf_op jit(solution)/shard_map/jit(cholesky)/cholesky | solution.py:24
  253.9 11.7 %cholesky.544 = f32[128,128]{1,0:T(8,128)S(1)} custom-call(f32[128,128]{1,0:T(8,128)S(1)} %cholesky.606), custom_call_target="Cholesky" | custom-call | tf_op jit(solution)/shard_map/jit(cholesky)/cholesky | solution.py:24
  267.5 10.2 %custom-call.68 = f32[1,128,128]{1,2,0:T(8,128)S(1)} custom-call(f32[1,128,128]{2,1,0:T(8,128)S(1)} %get-tuple-element.55), custom_call_target="InvertDiagBlocksLowerTriangular" | custom-call | tf_op jit(solution)/shard_map/jit(cholesky)/cholesky | solution.py:24
  280.4 11.7 %cholesky.562 = f32[128,128]{1,0:T(8,128)S(1)} custom-call(f32[128,128]{1,0:T(8,128)S(1)} %convolution_subtract_fusion.11), custom_call_target="Cholesky" | custom-call | tf_op jit(solution)/shard_map/jit(cholesky)/cholesky | solution.py:24
  298.8 22.5 %while.1 = (s32[]{:T(128)}, f32[1024,1024]{1,0:T(8,128)}, s32[8,2]{0,1:T(2,128)S(1)}, f32[8,128,128]{2,1,0:T(8,128)S(1)}, s32[]{:T(128)}) while((s32[]{:T(128)}, f32[1024,1024]{1,0:T(8,128)}, s32[8,2]{0,1:T(2,128)S(1)}, f32[8,128,128]{2,1,0:T(8,128)S(1)}, s32[]{:T(128)}) %tuple.61), condition=%wide.while_cond, body=%wide.while_body.sunk | while | flops 2 | bytes 131189 | solution.py:26
  321.2 78.8 %custom-call.69 = f32[8,128,128]{1,2,0:T(8,128)S(1)} custom-call(f32[8,128,128]{2,1,0:T(8,128)S(1)} %get-tuple-element.12), custom_call_target="InvertDiagBlocksLowerTriangular" | custom-call | tf_op jit(solution)/shard_map/triangular_solve | solution.py:26
  434.2 5.8 %convolution_subtract_fusion.1 = f32[2048,128]{0,1:T(8,128)S(1)} fusion(f32[2048,896]{0,1:T(8,128)S(1)} %get-tuple-element.27, f32[2048,1024]{0,1:T(8,128)S(1)} %bitcast.124, f32[1024,1024]{1,0:T(8,128)} %get-tuple-element.131), kind=kOutput, calls=%fused_computation.38 | convolution fusion | flops 2818834432 | bytes 9895936 | tf_op jit(solution)/shard_map/triangular_solve | solution.py:26
  444.3 38.9 %all-reduce.1 = (f32[1024]{0:T(1024)S(1)}, f32[1024]{0:T(1024)S(1)}) all-reduce(f32[1024]{0:T(1024)S(1)} %get-tuple-element.14, f32[1024]{0:T(1024)S(1)} %get-tuple-element.13), channel_id=1, replica_groups=mesh['grp'=4,'dev'=8] {'grp','dev'}, use_global_device_ids=true, to_apply=%region_22.23 | all-reduce | flops 2048 | bytes 16384 | tf_op jit(solution)/shard_map/psum | solution.py:28
  488.5 6.4 %copy.7 = bf16[2048,1024]{1,0:T(8,128)(2,1)} copy(bf16[2048,1024]{0,1:T(8,128)(2,1)} %divide_convert_fusion) | data formatting | bytes 8388608 | tf_op jit(solution)/shard_map/convert_element_type | solution.py:34
  (107 shorter events, 125.8 us)
Async XLA Ops:
  3.0 58.6 %copy-start.1 = (bf16[2048,256]{1,0:T(8,128)(2,1)S(1)}, bf16[2048,256]{1,0:T(8,128)(2,1)}, u32[]{:S(2)}) copy-start(bf16[2048,256]{1,0:T(8,128)(2,1)} %param.3) | copy-start | bytes 3145732
  76.9 5.4 %copy-start.5 = (f32[1024]{0:T(1024)S(1)}, f32[1024]{0:T(1024)}, u32[]{:S(2)}) copy-start(f32[1024]{0:T(1024)} %param.4) | copy-start | bytes 12292
  88.6 2.0 copy-start.2
  400.0 5.3 %copy-start.3 = (f32[8,128,128]{1,2,0:T(8,128)}, f32[8,128,128]{1,2,0:T(8,128)S(1)}, u32[]{:S(2)}) copy-start(f32[8,128,128]{1,2,0:T(8,128)S(1)} %custom-call.69) | copy-start | bytes 1572868
  400.0 6.6 %slice-start = ((s8[8388608]{0:T(1024)(128)(4,1)}), s8[4194304]{0:T(1024)(128)(4,1)S(1)}, s32[]{:S(2)}) async-start(s8[8388608]{0:T(1024)(128)(4,1)} %bitcast.123), calls=%async_computation | async-start | bytes 8388608
  402.8 3.8 slice-start.1
  406.6 2.3 copy-start.4
  441.0 3.2 copy-start
where the time goes:
time: 502 us; the launch traced here: 495 us
  other arithmetic  272 us (54%)
  blocking collectives  92.1 us (18%)
  matrix products  74 us (15%)
  local copies, waits for them, and re-layouts  51 us (10%)
  between operations  5.8 us (1%)
    another operation x30, other arithmetic, shards(): lower = jnp.linalg.cholesky(core)  172 us
    another operation x3, other arithmetic, shards(): lax.linalg.triangular_solve(lower, cross, left_side=False, lower=True, tr...  83.7 us
    psum x1, blocking collectives, shards(): marks = lax.psum(filled, ('grp', 'dev')).astype(jnp.bfloat16)  53.3 us
    another operation x15, matrix products, shards(): lax.linalg.triangular_solve(lower, cross, left_side=False, lower=True, tr...  40.8 us
    psum x1, blocking collectives, shards(): lax.psum((jnp.sum(raw, axis=0), jnp.sum(jnp.square(raw), axis=0)), ('grp'...  38.9 us
    another operation x14, matrix products, shards(): lower = jnp.linalg.cholesky(core)  23.2 us
    another operation x24, local copies, waits for them, and re-layouts  22.3 us

commit v1 on v0

--- a/solution.py
+++ b/solution.py
@@ -2,6 +2,11 @@
 import jax.numpy as jnp
 from jax import lax
 from jax.sharding import PartitionSpec as P
+
+
+def one_after_other(value, axis_one, axis_two):
+    partial = lax.psum(value, axis_one)
+    return lax.psum(partial, axis_two)
 
 
 def kernel_block(left, right):
@@ -25,8 +30,8 @@
     cross = kernel_block(points, marks)
     raw = lax.linalg.triangular_solve(lower, cross, left_side=False, lower=True, transpose_a=True)
     total_rows = count * lax.axis_size(("grp", "dev"))
-    totals, squares = lax.psum(
-        (jnp.sum(raw, axis=0), jnp.sum(jnp.square(raw), axis=0)), ("grp", "dev")
+    totals, squares = one_after_other(
+        (jnp.sum(raw, axis=0), jnp.sum(jnp.square(raw), axis=0)), "dev", "grp"
     )
     mean = totals / total_rows
     var = jnp.maximum(squares / total_rows - jnp.square(mean), 0.0)

time: 502 us -> 486 us (0.968)
  blocking collectives: 92.1 us -> 76.2 us
    psum x1 -> x2, blocking collectives: 38.9 us -> 22.9 us  [the longest x1 13.8 us: one_after_other(): partial = lax.psum(value, axis_one)]
where the time goes in v1:
time: 486 us; the launch traced here: 479 us
  other arithmetic  272 us (56%)
  blocking collectives  76.2 us (16%)
  matrix products  74 us (15%)
  local copies, waits for them, and re-layouts  51 us (10%)
  between operations  5.82 us (1%)
    another operation x30, other arithmetic, shards(): lower = jnp.linalg.cholesky(core)  172 us
    another operation x3, other arithmetic, shards(): lax.linalg.triangular_solve(lower, cross, left_side=False, lower=True, tr...  83.7 us
    psum x1, blocking collectives, shards(): marks = lax.psum(filled, ('grp', 'dev')).astype(jnp.bfloat16)  53.3 us
    another operation x15, matrix products, shards(): lax.linalg.triangular_solve(lower, cross, left_side=False, lower=True, tr...  40.8 us
    another operation x14, matrix products, shards(): lower = jnp.linalg.cholesky(core)  23.2 us
    another operation x24, local copies, waits for them, and re-layouts  22.3 us
    psum x1, blocking collectives, one_after_other(): partial = lax.psum(value, axis_one)  13.8 us
    dot_general x2, matrix products, kernel_block(): inner = jnp.dot(left, right.T, preferred_element_type=jnp.float32)  9.96 us

profile of v1, /device:TPU:0, one launch (start us, length us, event | category | flops | bytes accessed | tf_op | source)
XLA Modules:
  0.0 479.4 jit_solution(18303198051235936058)
XLA Ops:
  8.1 53.3 %all-reduce.4 = bf16[1024,256]{1,0:T(8,128)(2,1)S(1)} all-reduce(f32[1024,256]{1,0:T(8,128)S(1)} %convert_select_fusion), channel_id=1, replica_groups=mesh['grp'=4,'dev'=8] {'grp','dev'}, use_global_device_ids=true, to_apply=%region_1.2 | all-reduce | flops 262144 | bytes 1572864 | tf_op jit(solution)/shard_map/psum | solution.py:27
  66.0 5.6 %subtract_negate_fusion = (f32[1024,1024]{0,1:T(8,128)}, f32[1024,1024]{0,1:T(8,128)}, f32[1024,1024]{0,1:T(8,128)}) fusion(f32[1024]{0:T(1024)S(1)} %multiply_reduce_fusion.2, bf16[1024,256]{1,0:T(8,128)(2,1)S(1)} %all-reduce.4), kind=kOutput, calls=%fused_computation.27 | convolution fusion | flops 541065216 | bytes 13111296 | tf_op jit(solution)/shard_map/dot_general | solution.py:15
  82.3 6.3 %fusion.16 = f32[1024,1024]{1,0:T(8,128)S(1)} fusion(f32[1024,1024]{1,0:T(8,128)} %copy.6, f32[1024,1024]{1,0:T(8,128)} %copy.5, f32[1024,1024]{0,1:T(8,128)} %get-tuple-element.80, f32[1024]{0:T(1024)S(1)} %copy-done.5), kind=kLoop, calls=%fused_computation.24 | loop fusion | flops 13631488 | bytes 16781312 | tf_op jit(solution)/shard_map/jit(cholesky)/div | solution.py:29
  90.6 11.7 %cholesky.222 = f32[128,128]{1,0:T(8,128)S(1)} custom-call(f32[128,128]{1,0:T(8,128)S(1)} %cholesky.577), custom_call_target="Cholesky" | custom-call | tf_op jit(solution)/shard_map/jit(cholesky)/cholesky | solution.py:29
  102.4 9.8 %custom-call.62 = f32[1,128,128]{1,2,0:T(8,128)S(1)} custom-call(f32[1,128,128]{2,1,0:T(8,128)S(1)} %get-tuple-element.75), custom_call_target="InvertDiagBlocksLowerTriangular" | custom-call | tf_op jit(solution)/shard_map/jit(cholesky)/cholesky | solution.py:29
  118.6 11.7 %cholesky.243 = f32[128,128]{1,0:T(8,128)S(1)} custom-call(f32[128,128]{1,0:T(8,128)S(1)} %cholesky.581), custom_call_target="Cholesky" | custom-call | tf_op jit(solution)/shard_map/jit(cholesky)/cholesky | solution.py:29
  132.9 10.2 %custom-call.63 = f32[1,128,128]{1,2,0:T(8,128)S(1)} custom-call(f32[1,128,128]{2,1,0:T(8,128)S(1)} %get-tuple-element.72), custom_call_target="InvertDiagBlocksLowerTriangular" | custom-call | tf_op jit(solution)/shard_map/jit(cholesky)/cholesky | solution.py:29
  146.4 11.7 %cholesky.466 = f32[128,128]{1,0:T(8,128)S(1)} custom-call(f32[128,128]{1,0:T(8,128)S(1)} %cholesky.586), custom_call_target="Cholesky" | custom-call | tf_op jit(solution)/shard_map/jit(cholesky)/cholesky | solution.py:29
  160.1 9.8 %custom-call.64 = f32[1,128,128]{1,2,0:T(8,128)S(1)} custom-call(f32[1,128,128]{2,1,0:T(8,128)S(1)} %get-tuple-element.69), custom_call_target="InvertDiagBlocksLowerTriangular" | custom-call | tf_op jit(solution)/shard_map/jit(cholesky)/cholesky | solution.py:29
  173.4 11.9 %cholesky.485 = f32[128,128]{1,0:T(8,128)S(1)} custom-call(f32[128,128]{1,0:T(8,128)S(1)} %cholesky.591), custom_call_target="Cholesky" | custom-call | tf_op jit(solution)/shard_map/jit(cholesky)/cholesky | solution.py:29
  187.2 9.8 %custom-call.65 = f32[1,128,128]{1,2,0:T(8,128)S(1)} custom-call(f32[1,128,128]{2,1,0:T(8,128)S(1)} %get-tuple-element.66), custom_call_target="InvertDiagBlocksLowerTriangular" | custom-call | tf_op jit(solution)/shard_map/jit(cholesky)/cholesky | solution.py:29
  200.4 11.7 %cholesky.504 = f32[128,128]{1,0:T(8,128)S(1)} custom-call(f32[128,128]{1,0:T(8,128)S(1)} %cholesky.596), custom_call_target="Cholesky" | custom-call | tf_op jit(solution)/shard_map/jit(cholesky)/cholesky | solution.py:29
  214.0 9.8 %custom-call.66 = f32[1,128,128]{1,2,0:T(8,128)S(1)} custom-call(f32[1,128,128]{2,1,0:T(8,128)S(1)} %get-tuple-element.63), custom_call_target="InvertDiagBlocksLowerTriangular" | custom-call | tf_op jit(solution)/shard_map/jit(cholesky)/cholesky | solution.py:29
  227.4 11.7 %cholesky.524 = f32[128,128]{1,0:T(8,128)S(1)} custom-call(f32[128,128]{1,0:T(8,128)S(1)} %cholesky.601), custom_call_target="Cholesky" | custom-call | tf_op jit(solution)/shard_map/jit(cholesky)/cholesky | solution.py:29
  241.0 9.8 %custom-call.67 = f32[1,128,128]{1,2,0:T(8,128)S(1)} custom-call(f32[1,128,128]{2,1,0:T(8,128)S(1)} %get-tuple-element.60), custom_call_target="InvertDiagBlocksLowerTriangular" | custom-call | tf_op jit(solution)/shard_map/jit(cholesky)/cholesky | solution.py:29
  253.9 11.7 %cholesky.544 = f32[128,128]{1,0:T(8,128)S(1)} custom-call(f32[128,128]{1,0:T(8,128)S(1)} %cholesky.606), custom_call_target="Cholesky" | custom-call | tf_op jit(solution)/shard_map/jit(cholesky)/cholesky | solution.py:29
  267.5 10.2 %custom-call.68 = f32[1,128,128]{1,2,0:T(8,128)S(1)} custom-call(f32[1,128,128]{2,1,0:T(8,128)S(1)} %get-tuple-element.57), custom_call_target="InvertDiagBlocksLowerTriangular" | custom-call | tf_op jit(solution)/shard_map/jit(cholesky)/cholesky | solution.py:29
  280.3 11.7 %cholesky.562 = f32[128,128]{1,0:T(8,128)S(1)} custom-call(f32[128,128]{1,0:T(8,128)S(1)} %convolution_subtract_fusion.11), custom_call_target="Cholesky" | custom-call | tf_op jit(solution)/shard_map/jit(cholesky)/cholesky | solution.py:29
  298.8 22.5 %while.1 = (s32[]{:T(128)}, f32[1024,1024]{1,0:T(8,128)}, s32[8,2]{0,1:T(2,128)S(1)}, f32[8,128,128]{2,1,0:T(8,128)S(1)}, s32[]{:T(128)}) while((s32[]{:T(128)}, f32[1024,1024]{1,0:T(8,128)}, s32[8,2]{0,1:T(2,128)S(1)}, f32[8,128,128]{2,1,0:T(8,128)S(1)}, s32[]{:T(128)}) %tuple.61), condition=%wide.while_cond, body=%wide.while_body.sunk | while | flops 2 | bytes 131189 | solution.py:31
  321.2 78.8 %custom-call.69 = f32[8,128,128]{1,2,0:T(8,128)S(1)} custom-call(f32[8,128,128]{2,1,0:T(8,128)S(1)} %get-tuple-element.12), custom_call_target="InvertDiagBlocksLowerTriangular" | custom-call | tf_op jit(solution)/shard_map/triangular_solve | solution.py:31
  434.2 5.8 %convolution_subtract_fusion.1 = f32[2048,128]{0,1:T(8,128)S(1)} fusion(f32[2048,896]{0,1:T(8,128)S(1)} %get-tuple-element.29, f32[2048,1024]{0,1:T(8,128)S(1)} %bitcast.124, f32[1024,1024]{1,0:T(8,128)} %get-tuple-element.133), kind=kOutput, calls=%fused_computation.38 | convolution fusion | flops 2818834432 | bytes 9895936 | tf_op jit(solution)/shard_map/triangular_solve | solution.py:31
  444.3 13.8 %all-reduce.1 = (f32[1024]{0:T(1024)S(1)}, f32[1024]{0:T(1024)S(1)}) all-reduce(f32[1024]{0:T(1024)S(1)} %get-tuple-element.14, f32[1024]{0:T(1024)S(1)} %get-tuple-element.13), channel_id=1, replica_groups=mesh['grp'=4,'dev'=8] {'dev'}, use_global_device_ids=true, to_apply=%region_23.24 | all-reduce | flops 2048 | bytes 16384 | tf_op jit(solution)/shard_map/psum | solution.py:8
  458.1 9.1 %all-reduce.2 = (f32[1024]{0:T(1024)S(1)}, f32[1024]{0:T(1024)S(1)}) all-reduce(f32[1024]{0:T(1024)S(1)} %get-tuple-element.23, f32[1024]{0:T(1024)S(1)} %get-tuple-element.24), channel_id=1, replica_groups=mesh['grp'=4,'dev'=8] {'grp'}, use_global_device_ids=true, to_apply=%region_24.25 | all-reduce | flops 2048 | bytes 16384 | tf_op jit(solution)/shard_map/psum | solution.py:9
  472.5 6.4 %copy.7 = bf16[2048,1024]{1,0:T(8,128)(2,1)} copy(bf16[2048,1024]{0,1:T(8,128)(2,1)} %divide_convert_fusion) | data formatting | bytes 8388608 | tf_op jit(solution)/shard_map/convert_element_type | solution.py:39
  (108 shorter events, 131.1 us)
Async XLA Ops:
  3.0 58.6 %copy-start.1 = (bf16[2048,256]{1,0:T(8,128)(2,1)S(1)}, bf16[2048,256]{1,0:T(8,128)(2,1)}, u32[]{:S(2)}) copy-start(bf16[2048,256]{1,0:T(8,128)(2,1)} %param.3) | copy-start | bytes 3145732
  76.9 5.4 %copy-start.5 = (f32[1024]{0:T(1024)S(1)}, f32[1024]{0:T(1024)}, u32[]{:S(2)}) copy-start(f32[1024]{0:T(1024)} %param.4) | copy-start | bytes 12292
  88.6 2.0 copy-start.2
  400.0 5.3 %copy-start.3 = (f32[8,128,128]{1,2,0:T(8,128)}, f32[8,128,128]{1,2,0:T(8,128)S(1)}, u32[]{:S(2)}) copy-start(f32[8,128,128]{1,2,0:T(8,128)S(1)} %custom-call.69) | copy-start | bytes 1572868
  400.0 6.6 %slice-start = ((s8[8388608]{0:T(1024)(128)(4,1)}), s8[4194304]{0:T(1024)(128)(4,1)S(1)}, s32[]{:S(2)}) async-start(s8[8388608]{0:T(1024)(128)(4,1)} %bitcast.123), calls=%async_computation | async-start | bytes 8388608
  402.8 3.8 slice-start.1
  406.6 2.3 copy-start.4
  441.0 3.2 copy-start
